TPU v7x, 256 devices: a 2x2x32 block of a 4x8x32 slice. The times are simulated.
256 devices in a mesh: groups: 4 (over x, y), row: 64 (over z, core).
Axes of the slice: x: 2, y: 2, z: 32, core: 2. Of those that a mesh axis runs over, the one named last changes fastest.
The devices are a block of a 4x8x32 slice.
Arguments:
- factor_b: bfloat16 [64, 1048576], P(None, ('groups', 'row')), parts along dimension 1, may hold values from -12 to 12
- factor_c: bfloat16 [64, 1048576], P(None, ('groups', 'row')), parts along dimension 1, may hold values from -12 to 12
- sample_j: int32 [2097152], P(('groups', 'row')), parts along dimension 0, may hold values from 0 to 262143, as said below
- sample_k: int32 [64, 256, 128], P(None, ('groups', 'row')), parts along dimension 1, may hold values from 0 to 262143, as said below
- sample_weight: float32 [2097152], P(('groups', 'row')), parts along dimension 0, may hold values from 0.5 to 3.5
- block_values: bfloat16 [256, 64, 4, 4, 128], P(('groups', 'row')), parts along dimension 0, may hold values from -24 to 24
- block_sample: int32 [256, 64, 4, 4], P(('groups', 'row')), parts along dimension 0, may hold values from 0 to 8191
- block_count: int32 [256, 64, 4, 4], P(('groups', 'row')), parts along dimension 0, may hold values from 0 to 128, as said below
Outputs:
- factor_new: bfloat16 [64, 131072], P(None, ('groups', 'row')), parts along dimension 1
- scales: float32 [256], P('groups'), parts along dimension 0
There are 4 independent parts, one for each index of `groups`. A program takes and returns all parts, laid end to end along the dimension named above; each array names one. Nothing has to cross between parts.
Inputs may be any that keep to these rules, and one draw needn't show every extreme that they name: sample_j[s] lies in rows s // 8192 * 4096 to s // 8192 * 4096 + 4095. sample_k[d, e, i] is the third-mode index of sample d * 8192 + e * 128 + i and lies in rows e * 4096 to e * 4096 + 4095. `block_count`: 0 marks an empty slot; slot [p, p, 0, 0] holds 128 for every p.
All inputs are finite; a program needn't handle non-finite values.
Results may differ from a plain program's by a relative error of at most 0.0051.
Values may be sent and summed in bfloat16 or wider, within the bound.
A program may use at most 64 MiB of HBM per device.

v0:
```python
import jax
import jax.numpy as jnp
from jax import lax
from jax.sharding import Mesh
from jax.sharding import PartitionSpec as P

ROW = ("row_0", "row_1")
GROUPS_ROW = ("groups", "row_0", "row_1")


def by_axis(x, axes):
    for axis in axes:
        x = lax.psum(x, axis)
    return x


def sent_together(arrays, axis, split_dim, concat_dim, along):
    both = jnp.concatenate(arrays, axis=along)
    result, at, finished = (
        lax.all_to_all(both, axis, split_axis=split_dim, concat_axis=concat_dim, tiled=True),
        0,
        [],
    )
    for a in arrays:
        finished.append(lax.slice_in_dim(result, at, at + a.shape[along], axis=along))
        at += a.shape[along]
    return tuple(finished)


def from_everyone(x, axis):
    devices = lax.axis_size(axis)
    return lax.all_to_all(jnp.broadcast_to(x[None], (devices, *x.shape)), axis, 0, 0, tiled=True)


def over_copies(x, axis):
    return from_everyone(x, axis).sum(axis=0)


def shards(
    factor_b, factor_c, sample_j, sample_k, sample_weight, block_values, block_sample, block_count
):
    rank_width = factor_b.shape[0]
    device_count = lax.axis_size(ROW)
    device_index = lax.axis_index(ROW)
    b_columns = jnp.take(factor_b, sample_j - device_index * factor_b.shape[1], axis=1)
    c_local = sample_k.reshape(-1) - device_index * factor_c.shape[1]
    c_outgoing = jnp.take(factor_c, c_local, axis=1).reshape(rank_width, device_count, -1)
    c_columns = lax.all_to_all(c_outgoing, ROW, split_axis=1, concat_axis=1, tiled=True).reshape(
        rank_width, -1
    )
    sketch = sample_weight[None, :] * b_columns.astype(jnp.float32) * c_columns.astype(jnp.float32)
    gram_local = jnp.dot(sketch, sketch.T, precision=lax.Precision.HIGHEST)
    live_local = jnp.sum(block_count.astype(jnp.float32))
    gram_matrix, live_total = (by_axis(gram_local, ROW), by_axis(live_local, ROW))
    weighted = (sample_weight[None, :] * sketch).astype(jnp.bfloat16)
    positions = lax.broadcasted_iota(jnp.int32, block_values.shape, 4)
    masked = jnp.where(
        positions < block_count[..., None], block_values, jnp.zeros_like(block_values)
    )[0]
    tile_count = masked.shape[1]
    slot_count = masked.shape[2]
    weighted_rows = weighted.T
    picked = jnp.take(weighted_rows, block_sample.reshape(-1), axis=0)
    picked = picked.reshape(device_count, tile_count, slot_count, rank_width)
    values_in, rows_in = sent_together(
        (masked.reshape(device_count, -1), picked.reshape(device_count, -1)), ROW, 0, 0, 1
    )
    gathered = jnp.einsum(
        "stcr,stck->ktr",
        values_in.reshape(masked.shape),
        rows_in.reshape(picked.shape),
        preferred_element_type=jnp.float32,
    ).reshape(rank_width, -1)
    total_rows = gathered.shape[1] * device_count
    total_samples = sketch.shape[1] * device_count
    ridge = 0.05 * live_total / total_rows
    system = gram_matrix / total_samples + ridge * jnp.eye(rank_width, dtype=jnp.float32)
    lower_factor = jnp.linalg.cholesky(system)
    half_solved = lax.linalg.triangular_solve(lower_factor, gathered, left_side=True, lower=True)
    update = lax.linalg.triangular_solve(
        lower_factor, half_solved, left_side=True, lower=True, transpose_a=True
    )
    column_sums = over_copies(jnp.sum(update * update, axis=1), ROW)
    scales = jnp.sqrt(column_sums / total_rows + 1e-06)
    return ((update / scales[:, None]).astype(jnp.bfloat16), scales)


def solution(mesh):
    split = Mesh(mesh.devices.reshape(mesh.shape["groups"], 32, 2), ("groups", "row_0", "row_1"))
    return jax.shard_map(
        shards,
        mesh=split,
        in_specs=(
            P(None, GROUPS_ROW),
            P(None, GROUPS_ROW),
            P(GROUPS_ROW),
            P(None, GROUPS_ROW, None),
            P(GROUPS_ROW),
            P(GROUPS_ROW, None, None, None, None),
            P(GROUPS_ROW, None, None, None),
            P(GROUPS_ROW, None, None, None),
        ),
        out_specs=(P(None, GROUPS_ROW), P("groups")),
        check_vma=False,
    )
```

profile of v0, /device:TPU:37, one launch (start us, length us, event | category | flops | bytes accessed | tf_op | source)
XLA Modules:
  0.0 407.9 jit_solution(13769192548734777162)
XLA Ops:
  0.6 0.8 broadcast_subtract_fusion
  1.4 1.5 copy.61
  3.0 29.2 %gather_fusion.2 = bf16[8192,64]{1,0:T(8,128)(2,1)} fusion(bf16[64,4096]{0,1:T(8,128)(2,1)S(1)} %copy.61, s32[8192]{0:T(1024)S(1)} %fusion.11), kind=kCustom, calls=%fused_computation.1.clone | custom fusion | bytes 2129920 | tf_op jit(solution)/shard_map/jit(_take)/gather | solution.py:47
  32.2 5.8 %broadcast_select_fusion = bf16[8192,64]{1,0:T(8,128)(2,1)S(1)} fusion(bf16[8192,64]{1,0:T(8,128)(2,1)} %gather_fusion.2, pred[8192]{0:T(1024)(128)(4,1)S(1)} %compare_and_fusion), kind=kLoop, calls=%fused_computation.6 | loop fusion | flops 524288 | bytes 2105344 | tf_op jit(solution)/shard_map/jit(_take)/select_n | solution.py:47
  38.0 1.6 copy.62
  39.7 34.5 %all-to-all-start = ((bf16[64,64,128]{2,0,1:T(8,128)(2,1)}), bf16[64,64,128]{2,0,1:T(8,128)(2,1)S(1)}, u32[]{:S(2)}, u32[]{:S(2)}) async-start(bf16[64,64,128]{2,0,1:T(8,128)(2,1)} %copy.62), calls=%async_computation | async-start | bytes 2097152 | tf_op jit(solution)/shard_map/all_to_all | solution.py:48
  74.2 0.5 copy.60
  75.3 0.2 broadcast_in_dim.38
  75.7 0.3 fusion.1
  76.2 29.2 %gather_fusion.1 = bf16[8192,64]{1,0:T(8,128)(2,1)} fusion(bf16[64,4096]{0,1:T(8,128)(2,1)S(1)} %copy.60, s32[8192]{0:T(1024)S(1)} %fusion.12), kind=kCustom, calls=%fused_computation.clone | custom fusion | bytes 2129920 | tf_op jit(solution)/shard_map/jit(_take)/gather | solution.py:45
  105.5 76.1 %all-to-all-done = bf16[64,64,128]{2,0,1:T(8,128)(2,1)S(1)} async-done(((bf16[64,64,128]{2,0,1:T(8,128)(2,1)}), bf16[64,64,128]{2,0,1:T(8,128)(2,1)S(1)}, u32[]{:S(2)}, u32[]{:S(2)}) %all-to-all-start) | async-done | bytes 1048608 | tf_op jit(solution)/shard_map/all_to_all | solution.py:48
  181.6 2.4 copy.63
  184.0 10.4 %fusion = (bf16[8192,64]{1,0:T(8,128)(2,1)S(1)}, f32[64,8192]{0,1:T(8,128)}) fusion(f32[8192]{0:T(1024)S(1)} %copy-done.3, f32[64,64,128]{0,2,1:T(8,128)} %copy.63, bf16[8192,64]{1,0:T(8,128)(2,1)} %gather_fusion.1, pred[8192]{0:T(1024)(128)(4,1)S(1)} %compare_and_fusion.1), kind=kLoop, calls=%fused_computation.5 | loop fusion | flops 3145728 | bytes 6332416 | tf_op jit(solution)/shard_map/transpose | solution.py:62
  194.3 3.2 gather_fusion
  197.8 0.5 broadcast.154
  198.3 0.9 reduce.7
  199.2 1.0 reshape.144
  200.2 7.9 %all-to-all-start.1 = ((bf16[64,2,1536]{2,1,0:T(2,128)(2,1)}), bf16[64,2,1536]{2,1,0:T(2,128)(2,1)S(1)}, u32[]{:S(2)}, u32[]{:S(2)}) async-start(bf16[64,2,1536]{2,1,0:T(2,128)(2,1)} %reshape.144), calls=%async_computation.1 | async-start | bytes 786432 | tf_op jit(solution)/shard_map/all_to_all | solution.py:20
  208.2 0.6 convert_reduce_fusion
  208.8 10.4 %fusion.13 = f32[64,64]{1,0:T(8,128)S(1)} fusion(f32[64,8192]{0,1:T(8,128)} %get-tuple-element.8), kind=kOutput, calls=%fused_computation.44 | convolution fusion | flops 402653184 | bytes 2113536 | tf_op jit(solution)/shard_map/dot_general | solution.py:52
  219.2 101.2 %all-reduce = (f32[64,64]{1,0:T(8,128)S(1)}, f32[]{:T(128)}) all-reduce(f32[64,64]{1,0:T(8,128)S(1)} %fusion.13, f32[]{:T(128)} %convert_reduce_fusion), channel_id=1, replica_groups=mesh['groups'=4,'row_0'=32,'row_1'=2] {'row_0'}, use_global_device_ids=true, to_apply=%region_0.0 | all-reduce | flops 4097 | bytes 32776 | tf_op jit(solution)/shard_map/psum | solution.py:13
  320.4 30.4 %all-reduce.1 = (f32[64,64]{1,0:T(8,128)S(1)}, f32[]{:T(128)}) all-reduce(f32[64,64]{1,0:T(8,128)S(1)} %get-tuple-element.3, f32[]{:T(128)} %get-tuple-element.4), channel_id=1, replica_groups=mesh['groups'=4,'row_0'=32,'row_1'=2] {'row_1'}, use_global_device_ids=true, to_apply=%region_1.3 | all-reduce | flops 4097 | bytes 32776 | tf_op jit(solution)/shard_map/psum | solution.py:13
  351.6 5.8 %cholesky.16 = f32[64,64]{1,0:T(8,128)S(1)} custom-call(f32[64,64]{1,0:T(8,128)S(1)} %fusion.10), custom_call_target="Cholesky" | custom-call | tf_op jit(solution)/shard_map/jit(cholesky)/cholesky | solution.py:78
  357.4 0.6 compare_reduce_fusion
  358.1 0.7 fusion.6
  358.7 4.9 %custom-call.8 = f32[1,64,64]{1,2,0:T(8,128)S(1)} custom-call(f32[1,64,64]{2,1,0:T(8,128)S(1)} %fusion.6), custom_call_target="InvertDiagBlocksLowerTriangular" | custom-call | tf_op jit(solution)/shard_map/triangular_solve | solution.py:80
  363.7 0.3 reshape.145
  364.5 0.2 convolution_bitcast_fusion
  364.8 0.3 fusion.3
  365.1 0.4 multiply_reduce_fusion
  365.5 41.7 %all_to_all.23 = f32[64,1,64]{2,1,0:T(1,128)S(1)} all-to-all(f32[64,1,64]{2,1,0:T(1,128)S(1)} %broadcast_in_dim.40), channel_id=1, replica_groups=mesh['groups'=4,'row_0'=32,'row_1'=2] {'row_0','row_1'}, dimensions={0} | all-to-all | bytes 32768 | tf_op jit(solution)/shard_map/all_to_all | solution.py:32
  407.2 0.7 divide_convert_fusion
  (43 shorter events, 2.0 us)
Async XLA Ops:
  38.0 36.1 %copy-start = (bf16[64,4096]{1,0:T(8,128)(2,1)S(1)}, bf16[64,4096]{1,0:T(8,128)(2,1)}, u32[]{:S(2)}) copy-start(bf16[64,4096]{1,0:T(8,128)(2,1)} %param.10) | copy-start | bytes 1572868
  39.7 35.0 %copy-start.4 = (s32[1,64,4,4]{1,3,2,0:T(4,128)S(1)}, s32[1,64,4,4]{1,3,2,0:T(4,128)}, u32[]{:S(2)}) copy-start(s32[1,64,4,4]{1,3,2,0:T(4,128)} %param.16) | copy-start | bytes 12292
  39.7 35.8 %copy-start.5 = (s32[1,64,4,4]{1,3,2,0:T(4,128)S(1)}, s32[1,64,4,4]{1,3,2,0:T(4,128)}, u32[]{:S(2)}) copy-start(s32[1,64,4,4]{1,3,2,0:T(4,128)} %param.17) | copy-start | bytes 12292
  39.7 36.0 %copy-start.1 = (bf16[1,64,4,4,128]{4,3,2,1,0:T(4,128)(2,1)S(1)}, bf16[1,64,4,4,128]{4,3,2,1,0:T(4,128)(2,1)}, u32[]{:S(2)}) copy-start(bf16[1,64,4,4,128]{4,3,2,1,0:T(4,128)(2,1)} %param.15) | copy-start | bytes 786436
  39.7 141.9 %all-to-all-start = ((bf16[64,64,128]{2,0,1:T(8,128)(2,1)}), bf16[64,64,128]{2,0,1:T(8,128)(2,1)S(1)}, u32[]{:S(2)}, u32[]{:S(2)}) async-start(bf16[64,64,128]{2,0,1:T(8,128)(2,1)} %copy.62), calls=%async_computation | async-start | bytes 2097152 | tf_op jit(solution)/shard_map/all_to_all | solution.py:48
  74.2 2.0 copy-start.2
  105.5 78.5 %copy-start.3 = (f32[8192]{0:T(1024)S(1)}, f32[8192]{0:T(1024)}, u32[]{:S(2)}) copy-start(f32[8192]{0:T(1024)} %param.14) | copy-start | bytes 98308
  200.2 163.4 %all-to-all-start.1 = ((bf16[64,2,1536]{2,1,0:T(2,128)(2,1)}), bf16[64,2,1536]{2,1,0:T(2,128)(2,1)S(1)}, u32[]{:S(2)}, u32[]{:S(2)}) async-start(bf16[64,2,1536]{2,1,0:T(2,128)(2,1)} %reshape.144), calls=%async_computation.1 | async-start | bytes 786432 | tf_op jit(solution)/shard_map/all_to_all | solution.py:20
  407.2 0.7 copy-start.6
where the time goes:
time: 409 us; the launch traced here: 408 us
  blocking collectives  173 us (42%)
  waiting for transfers between devices  76.1 us (19%)
  local copies, waits for them, and re-layouts  71.5 us (17%)
  starting transfers between devices  42.4 us (10%)
  other arithmetic  31.7 us (8%)
  matrix products  11.3 us (3%)
    psum x2, blocking collectives, by_axis(): x = lax.psum(x, axis)  132 us
    all_to_all x1, waiting for transfers between devices, shards(): lax.all_to_all(c_outgoing, ROW, split_axis=1, concat_axis=1, tiled=True)  76.1 us
    all_to_all x1, blocking collectives, from_everyone(): lax.all_to_all(jnp.broadcast_to(x[None], (devices, *x.shape)), axis, 0, 0...  41.7 us
    all_to_all x1, starting transfers between devices, shards(): lax.all_to_all(c_outgoing, ROW, split_axis=1, concat_axis=1, tiled=True)  34.5 us
    gather x1, local copies, waits for them, and re-layouts, shards(): jnp.take(factor_c, c_local, axis=1).reshape(rank_width, device_count, -1)  29.2 us
    gather x1, local copies, waits for them, and re-layouts, shards(): jnp.take(factor_b, sample_j - device_index * factor_b.shape[1], axis=1)  29.2 us
    dot_general x1, matrix products, shards(): gram_local = jnp.dot(sketch, sketch.T, precision=lax.Precision.HIGHEST)  10.4 us
    transpose x1, other arithmetic, shards(): weighted_rows = weighted.T  10.4 us
  transfers between devices with their start and end apart: 2, of which 1 were waited for; matrix products, arithmetic and copies ran while one was open for 13% of the time, Pallas kernels for 0%

commit v1 on v0

v1 whole, which is shorter than its diff:
```python
import functools

import jax
import jax.numpy as jnp
from jax import lax
from jax.experimental import pallas as pl
from jax.experimental.pallas import tpu as pltpu
from jax.sharding import PartitionSpec as P

MESH = pl.DeviceIdType.MESH
GROUPS_ROW = ("groups", "row")
HIGHEST = lax.Precision.HIGHEST
F32 = jnp.float32
BF16 = jnp.bfloat16


def partner(step, me, n, sign):
    chips = n // 2
    z, core = me // 2, me % 2
    rest = step - 2
    dist = jnp.where(step < 2, chips // 2, chips // 2 - 1 - rest // 4)
    way = jnp.where(step < 2, 1, 1 - 2 * ((rest // 2) % 2)) * sign
    other = jnp.where(step < 2, step, rest % 2)
    other = jnp.where(step == n - 2, 1 - core, other)
    return lax.rem(z + dist * way + chips, chips) * 2 + other


def send(src, dst, send_sem, recv_sem, peer):
    copy = pltpu.make_async_remote_copy(
        src_ref=src,
        dst_ref=dst,
        send_sem=send_sem,
        recv_sem=recv_sem,
        device_id={"row": peer},
        device_id_type=MESH,
    )
    copy.start()


def arrived(ref, send_sem, recv_sem, peer):
    pltpu.make_async_remote_copy(
        src_ref=ref, dst_ref=ref, send_sem=send_sem, recv_sem=recv_sem, device_id={"row": peer}, device_id_type=MESH
    ).wait_recv()


def sent(ref, send_sem, recv_sem, peer):
    pltpu.make_async_remote_copy(
        src_ref=ref, dst_ref=ref, send_sem=send_sem, recv_sem=recv_sem, device_id={"row": peer}, device_id_type=MESH
    ).wait_send()


def kernel(
    n,
    total_samples,
    total_rows,
    k_ref,
    j_ref,
    pick_ref,
    live_ref,
    b_ref,
    c_ref,
    w_ref,
    values_ref,
    out_ref,
    scales_ref,
    table_c,
    table_b,
    stage,
    c_out,
    c_in,
    wb,
    wp,
    wk,
    values_in,
    rows_out,
    rows_in,
    g_out,
    g_one,
    g_mid,
    g_two,
    g_sum,
    g_all,
    s_out,
    s_one,
    s_mid,
    s_two,
    c_send,
    c_recv,
    v_send,
    v_recv,
    r_send,
    r_recv,
    small_send,
    small_recv,
):
    me = lax.axis_index("row")
    rank = b_ref.shape[0]
    depth_c, depth_b = c_ref.shape[1], b_ref.shape[1]
    per = k_ref.shape[0] // n
    half = per // 2
    side = 8
    assert depth_c & (depth_c - 1) == 0 and depth_b & (depth_b - 1) == 0
    ring, seat = me // side, me % side
    lane = lax.broadcasted_iota(jnp.int32, (1, 128), 1)
    left = lane < rank

    barrier = pltpu.get_barrier_semaphore()

    def greet(i, _):
        pl.semaphore_signal(barrier, inc=1, device_id={"row": partner(i, me, n, 1)}, device_id_type=MESH)
        return 0

    lax.fori_loop(0, n - 1, greet, 0)

    def fill(table, ref):
        def chunk(i, _):
            at = pl.multiple_of(i * 128, 128)
            part = ref[:, pl.ds(at, 128)].astype(F32).T
            table[pl.ds(at, 128), :] = jnp.concatenate([part, part], axis=1)
            return 0

        lax.fori_loop(0, ref.shape[1] // 128, chunk, 0)

    def rows_of(table, index_ref, at, mask):
        for i in range(half):
            first = table[pl.ds(index_ref[at + i] & mask, 1), :]
            second = table[pl.ds(index_ref[at + half + i] & mask, 1), :]
            stage[i : i + 1, :] = jnp.where(left, first, second)
        return stage[...]

    fill(table_c, c_ref)

    def gather_c(i, _):
        peer = jnp.where(i == n - 1, me, partner(i, me, n, 1))
        c_out[peer] = rows_of(table_c, k_ref, peer * per, depth_c - 1).astype(BF16)
        return 0

    early = n // 2
    lax.fori_loop(0, early, gather_c, 0)

    pl.semaphore_wait(barrier, n - 1)

    def send_values(i, _):
        peer = partner(i, me, n, 1)
        send(values_ref.at[peer], values_in.at[me], v_send.at[peer], v_recv.at[me], peer)
        return 0

    lax.fori_loop(0, n - 1, send_values, 0)
    lax.fori_loop(early, n, gather_c, 0)

    def send_c(i, _):
        peer = partner(i, me, n, 1)
        send(c_out.at[peer], c_in.at[me], c_send.at[peer], c_recv.at[me], peer)
        return 0

    lax.fori_loop(0, n - 1, send_c, 0)
    values_in[me] = values_ref[me]

    fill(table_b, b_ref)

    def weigh(i, _):
        turned = w_ref[pl.ds(pl.multiple_of(i * 8, 8), 8), :].T
        for j in range(8):
            wp[i * 8 + j] = jnp.where(left, turned[:half, j : j + 1], turned[half:, j : j + 1])
        return 0

    lax.fori_loop(0, n // 8, weigh, 0)

    def gather_b(e, _):
        wb[e] = rows_of(table_b, j_ref, e * per, depth_b - 1) * wp[e]
        return 0

    lax.fori_loop(0, n, gather_b, 0)

    def use(e, c_rows, gram):
        sketch = wb[e] * c_rows.astype(F32)
        weighted = wp[e] * sketch
        turned = pltpu.roll(weighted, rank, 1)
        at = pl.multiple_of(e * per, 128)
        wk[pl.ds(at, half), :] = jnp.where(left, weighted, turned)
        wk[pl.ds(at + half, half), :] = jnp.where(left, turned, weighted)
        return gram + lax.dot_general(
            sketch, sketch, (((0,), (0,)), ((), ())), precision=HIGHEST, preferred_element_type=F32
        )

    gram = use(me, c_out[me], jnp.zeros((128, 128), F32))

    def take(i, gram):
        e = partner(i, me, n, -1)
        arrived(c_in.at[e], c_send.at[e], c_recv.at[e], e)
        return use(e, c_in[e], gram)

    gram = lax.fori_loop(0, n - 1, take, gram)

    eye = lax.broadcasted_iota(jnp.int32, (rank, 128), 0) == lax.broadcasted_iota(jnp.int32, (rank, 128), 1)
    square = gram[:rank, :rank] + gram[rank:, rank:]
    ridge = (0.05 / total_rows) * live_ref[0]
    system = square * (1.0 / total_samples) + jnp.where(eye[:, :rank], ridge, 0.0)
    packed = jnp.concatenate([system[: rank // 2], system[rank // 2 :]], axis=1)
    lines = packed.shape[0] // side
    for i in range(side):
        g_out[i] = packed[i * lines : (i + 1) * lines]
    g_one[seat] = g_out[seat]

    def spread(kind, src_of, dst, peer_of, own):
        for j in range(1, side):
            peer, index = peer_of(j)
            send(src_of(index), dst.at[own], small_send.at[kind, index], small_recv.at[kind, own], peer)

    def collect(kind, dst, peer_of):
        for j in range(1, side):
            peer, index = peer_of(j)
            arrived(dst.at[index], small_send.at[kind, index], small_recv.at[kind, index], peer)

    def in_ring(j):
        index = lax.rem(seat + j, side)
        return ring * side + index, index

    def across(j):
        index = lax.rem(ring + j, side)
        return index * side + seat, index

    spread(0, lambda i: g_out.at[i], g_one, in_ring, seat)

    def pick(q, _):
        at = q * 16
        for i in range(8):
            first = wk[pl.ds(pick_ref[at + i], 1), :]
            second = wk[pl.ds(pick_ref[at + 8 + i], 1), :]
            stage[i : i + 1, :] = jnp.where(left, first, second)
        rows_out[q] = stage[0:8, :].astype(BF16)
        return 0

    lax.fori_loop(0, n, pick, 0)

    collect(0, g_one, in_ring)
    total = g_one[0]
    for i in range(1, side):
        total = total + g_one[i]
    g_mid[...] = total
    g_two[ring] = total
    spread(1, lambda i: g_mid, g_two, across, ring)

    def send_rows(i, _):
        peer = partner(i, me, n, 1)
        send(rows_out.at[peer], rows_in.at[me], r_send.at[peer], r_recv.at[me], peer)
        return 0

    lax.fori_loop(0, n - 1, send_rows, 0)
    rows_in[me] = rows_out[me]

    collect(1, g_two, across)
    total = g_two[0]
    for i in range(1, side):
        total = total + g_two[i]
    g_sum[...] = total
    g_all[seat] = total
    spread(2, lambda i: g_sum, g_all, in_ring, seat)
    collect(2, g_all, in_ring)
    packed = jnp.concatenate([g_all[i] for i in range(side)], axis=0)
    matrix = jnp.concatenate([packed, pltpu.roll(packed, rank, 1)], axis=0)
    matrix = jnp.where(left, matrix, pltpu.roll(matrix, rank, 1))

    row_at = lax.broadcasted_iota(jnp.int32, (rank, 1), 0)
    lane_at = lax.rem(lane, rank)

    def eliminate(_, m):
        for i in range(8):
            column = m[:, i : i + 1]
            inverse = 1.0 / m[i : i + 1, i : i + 1]
            line = jnp.where(lane_at == i, 1.0, m[i : i + 1, :]) * inverse
            rest = jnp.where(lane_at == i, 0.0, m) - column * line
            m = jnp.where(row_at == i, line, rest)
        m = pltpu.roll(m, 120, 1)
        return jnp.concatenate([m[8:], m[:8]], axis=0)

    inverse = lax.fori_loop(0, rank // 8, eliminate, matrix)[:, :rank]

    def wait_blocks(i, _):
        e = partner(i, me, n, -1)
        arrived(values_in.at[e], v_send.at[e], v_recv.at[e], e)
        arrived(rows_in.at[e], r_send.at[e], r_recv.at[e], e)
        return 0

    lax.fori_loop(0, n - 1, wait_blocks, 0)

    rows = rows_in[...].astype(F32).reshape(n * 8, 128)
    low = values_in[:, 0].astype(F32).reshape(n * 8, 128).astype(BF16)
    high = values_in[:, 1].astype(F32).reshape(n * 8, 128).astype(BF16)
    slot = lax.rem(lax.broadcasted_iota(jnp.int32, (n * 8, 1), 0), 8)

    def mixed(mask, values):
        return lax.dot_general(
            jnp.where(mask, rows, 0.0).astype(BF16), values, (((0,), (0,)), ((), ())), preferred_element_type=F32
        )

    gathered = [
        mixed(slot < 4, low)[:rank],
        mixed(slot >= 4, low)[:rank],
        mixed(slot < 4, high)[rank:],
        mixed(slot >= 4, high)[rank:],
    ]
    update = [
        lax.dot_general(inverse, g, (((1,), (0,)), ((), ())), precision=HIGHEST, preferred_element_type=F32)
        for g in gathered
    ]
    squares = update[0] * update[0]
    for u in update[1:]:
        squares = squares + u * u
    own = jnp.sum(squares, axis=1, keepdims=True)
    own = jnp.sum(jnp.where(eye, own, 0.0), axis=0, keepdims=True)
    s_out[...] = own
    s_one[seat] = own
    spread(3, lambda i: s_out, s_one, in_ring, seat)
    collect(3, s_one, in_ring)
    total = s_one[0]
    for i in range(1, side):
        total = total + s_one[i]
    s_mid[...] = total
    s_two[ring] = total
    spread(4, lambda i: s_mid, s_two, across, ring)
    collect(4, s_two, across)
    total = s_two[0]
    for i in range(1, side):
        total = total + s_two[i]
    scales = jnp.sqrt(total / total_rows + 1e-06)
    scales_ref[...] = scales
    column = jnp.sum(jnp.where(eye, scales, 0.0), axis=1, keepdims=True)
    for t, u in enumerate(update):
        out_ref[:, t * 128 : (t + 1) * 128] = (u / column).astype(BF16)

    def drain(i, _):
        peer = partner(i, me, n, 1)
        sent(values_ref.at[peer], v_send.at[peer], v_recv.at[peer], peer)
        sent(c_out.at[peer], c_send.at[peer], c_recv.at[peer], peer)
        sent(rows_out.at[peer], r_send.at[peer], r_recv.at[peer], peer)
        return 0

    lax.fori_loop(0, n - 1, drain, 0)
    for kind, ref, peer_of in (
        (0, g_out.at[0], in_ring),
        (1, g_mid, across),
        (2, g_sum, in_ring),
        (3, s_out, in_ring),
        (4, s_mid, across),
    ):
        for j in range(1, side):
            peer, index = peer_of(j)
            sent(ref, small_send.at[kind, index], small_recv.at[kind, index], peer)


def solution(mesh):
    n = mesh.shape["row"]

    def shards(
        factor_b, factor_c, sample_j, sample_k, sample_weight, block_values, block_sample, block_count
    ):
        rank = factor_b.shape[0]
        samples = sample_j.shape[0]
        _, _, tiles, slots, width = block_values.shape
        positions = lax.broadcasted_iota(jnp.int32, block_values.shape, 4)
        masked = jnp.where(positions < block_count[..., None], block_values, jnp.zeros_like(block_values))
        masked = masked.reshape(n, 2, tiles * slots // 2, width)
        live = jnp.sum(block_count.astype(F32)).reshape(1)
        vmem = pl.BlockSpec(memory_space=pltpu.VMEM)
        smem = pl.BlockSpec(memory_space=pltpu.SMEM)
        half = samples // n // 2
        out, scales = pl.pallas_call(
            functools.partial(kernel, n, samples * n, tiles * width * n),
            out_shape=(
                jax.ShapeDtypeStruct((rank, tiles * width), BF16),
                jax.ShapeDtypeStruct((1, 128), F32),
            ),
            in_specs=[smem] * 4 + [vmem] * 4,
            out_specs=(vmem, vmem),
            scratch_shapes=[
                pltpu.VMEM((factor_c.shape[1], 128), F32),
                pltpu.VMEM((factor_b.shape[1], 128), F32),
                pltpu.VMEM((half, 128), F32),
                pltpu.VMEM((n, half, 128), BF16),
                pltpu.VMEM((n, half, 128), BF16),
                pltpu.VMEM((n, half, 128), F32),
                pltpu.VMEM((n, half, 128), F32),
                pltpu.VMEM((samples, 128), F32),
                pltpu.VMEM(masked.shape, BF16),
                pltpu.VMEM((n, 8, 128), BF16),
                pltpu.VMEM((n, 8, 128), BF16),
                pltpu.VMEM((8, 4, 128), F32),
                pltpu.VMEM((8, 4, 128), F32),
                pltpu.VMEM((4, 128), F32),
                pltpu.VMEM((8, 4, 128), F32),
                pltpu.VMEM((4, 128), F32),
                pltpu.VMEM((8, 4, 128), F32),
                pltpu.VMEM((1, 128), F32),
                pltpu.VMEM((8, 1, 128), F32),
                pltpu.VMEM((1, 128), F32),
                pltpu.VMEM((8, 1, 128), F32),
            ]
            + [pltpu.SemaphoreType.DMA((n,))] * 6
            + [pltpu.SemaphoreType.DMA((5, 8))] * 2,
            compiler_params=pltpu.CompilerParams(collective_id=0, has_side_effects=True),
            name="step",
        )(
            sample_k.reshape(-1),
            sample_j,
            block_sample.reshape(-1),
            live,
            factor_b,
            factor_c,
            sample_weight.reshape(n, -1),
            masked,
        )
        return out, scales[0, :rank]

    return jax.shard_map(
        shards,
        mesh=mesh,
        in_specs=(
            P(None, GROUPS_ROW),
            P(None, GROUPS_ROW),
            P(GROUPS_ROW),
            P(None, GROUPS_ROW, None),
            P(GROUPS_ROW),
            P(GROUPS_ROW, None, None, None, None),
            P(GROUPS_ROW, None, None, None),
            P(GROUPS_ROW, None, None, None),
        ),
        out_specs=(P(None, GROUPS_ROW), P("groups")),
        check_vma=False,
    )
```

time: 409 us -> 212 us (0.52)
  Pallas kernels: 0 us -> 204 us
  blocking collectives: 173 us -> 0 us
  waiting for transfers between devices: 76.1 us -> 0 us
  local copies, waits for them, and re-layouts: 71.5 us -> 4.3 us
  starting transfers between devices: 42.4 us -> 0 us
  other arithmetic: 31.7 us -> 2.58 us
  matrix products: 11.3 us -> 0 us
    pallas_call x0 -> x1, Pallas kernels: none -> 204 us  [shards(): pl.pallas_call(functools.partial(kernel, n, samples * n, tiles * width *...]
    psum x2 -> x0, blocking collectives: 132 us -> none  [by_axis(): x = lax.psum(x, axis)]
    all_to_all x2 -> x0, waiting for transfers between devices: 76.1 us -> none  [the longest x1 76.1 us: shards(): lax.all_to_all(c_outgoing, ROW, split_axis=1, concat_axis=1, tiled=True)]
    gather x4 -> x0, local copies, waits for them, and re-layouts: 61.8 us -> none  [the longest x1 29.2 us: shards(): jnp.take(factor_c, c_local, axis=1).reshape(rank_width, device_count, -1)]
    all_to_all x2 -> x0, starting transfers between devices: 42.4 us -> none  [the longest x1 34.5 us: shards(): lax.all_to_all(c_outgoing, ROW, split_axis=1, concat_axis=1, tiled=True)]
    all_to_all x1 -> x0, blocking collectives: 41.7 us -> none  [from_everyone(): lax.all_to_all(jnp.broadcast_to(x[None], (devices, *x.shape)), axis, 0, 0...]
    another operation x5 -> x0, other arithmetic: 12.1 us -> none  [the longest x3 6.52 us: shards(): lower_factor = jnp.linalg.cholesky(system)]
    dot_general x2 -> x0, matrix products: 10.7 us -> none  [the longest x1 10.4 us: shards(): gram_local = jnp.dot(sketch, sketch.T, precision=lax.Precision.HIGHEST)]
  transfers between devices with their start and end apart: 2 -> 0, of which waited for: 1 -> 0; matrix products, arithmetic and copies ran while one was open for 13% -> 0% of each run, Pallas kernels for 0% -> 0%
where the time goes in v1:
time: 212 us; the launch traced here: 211 us
  Pallas kernels  204 us (96%)
  local copies, waits for them, and re-layouts  4.3 us (2%)
  other arithmetic  2.58 us (1%)
    pallas_call x1, Pallas kernels, shards(): pl.pallas_call(functools.partial(kernel, n, samples * n, tiles * width *...  204 us

profile of v1, /device:TPU:37, one launch (start us, length us, event | category | flops | bytes accessed | tf_op | source)
XLA Modules:
  0.0 211.5 jit_solution(16369738175696664919)
XLA Ops:
  0.6 0.8 copy.12
  1.5 0.0 copy-start.1
  1.5 2.0 fusion
  3.5 0.0 copy-done.1
  3.5 0.1 copy.11
  3.6 0.0 copy-start
  3.6 0.8 reshape.31.pick_ref
  4.4 0.0 copy-done
  4.4 0.6 convert_reduce_fusion
  5.0 203.9 %step.1 = (bf16[64,512]{1,0:T(8,128)(2,1)}, f32[1,128]{1,0:T(1,128)}) custom-call(s32[8192]{0:T(1024)} %bitcast.8, s32[8192]{0:T(1024)} %j_ref.1, s32[1024]{0:T(1024)} %reshape.31.pick_ref, f32[1]{0:T(128)} %bitcast.1.live_ref, bf16[64,4096]{1,0:T(8,128)(2,1)} %b_ref.1, bf16[64,4096]{1,0:T(8,128)(2,1)} %c_ref.1, f32[64,128]{1,0:T(8,128)} %bitcast.9, ...), custom_call_target="tpu_custom_call" | custom-call | tf_op jit(solution)/shard_map/step/pallas_call | solution.py:368
  208.9 0.0 copy-start.2
  208.9 0.6 copy-done.2
  209.5 0.5 slice_bitcast_fusion
  210.0 1.5 copy.14
Async XLA Ops:
  1.5 2.0 copy-start.1
  3.6 0.8 copy-start
  208.9 0.6 copy-start.2

commit v2 on v1

v2 whole, which is shorter than its diff:
```python
import functools

import jax
import jax.numpy as jnp
from jax import lax
from jax.experimental import pallas as pl
from jax.experimental.pallas import tpu as pltpu
from jax.sharding import PartitionSpec as P

MESH = pl.DeviceIdType.MESH
GROUPS_ROW = ("groups", "row")
HIGHEST = lax.Precision.HIGHEST
F32 = jnp.float32
BF16 = jnp.bfloat16


def partner(step, me, n, sign):
    chips = n // 2
    z, core = me // 2, me % 2
    rest = step - 2
    dist = jnp.where(step < 2, chips // 2, chips // 2 - 1 - rest // 4)
    way = jnp.where(step < 2, 1, 1 - 2 * ((rest // 2) % 2)) * sign
    other = jnp.where(step < 2, step, rest % 2)
    other = jnp.where(step == n - 2, 1 - core, other)
    return lax.rem(z + dist * way + chips, chips) * 2 + other


def send(src, dst, send_sem, recv_sem, peer):
    copy = pltpu.make_async_remote_copy(
        src_ref=src,
        dst_ref=dst,
        send_sem=send_sem,
        recv_sem=recv_sem,
        device_id={"row": peer},
        device_id_type=MESH,
    )
    copy.start()


def wait_blocks(ref, send_sem, recv_sem, peer, incoming):
    copy = pltpu.make_async_remote_copy(
        src_ref=ref, dst_ref=ref, send_sem=send_sem, recv_sem=recv_sem, device_id={"row": peer}, device_id_type=MESH
    )
    if incoming:
        copy.wait_recv()
    else:
        copy.wait_send()


def kernel(
    n,
    total_samples,
    total_rows,
    k_hbm,
    j_hbm,
    pick_hbm,
    count_hbm,
    b_hbm,
    c_hbm,
    w_hbm,
    values_hbm,
    update_hbm,
    scales_ref,
    k_ref,
    j_ref,
    pick_ref,
    count_ref,
    b_ref,
    c_ref,
    w_ref,
    values_ref,
    table_c,
    table_b,
    stage,
    c_out,
    c_in,
    wb,
    wp,
    wk,
    values_out,
    values_in,
    rows_out,
    rows_in,
    g_out,
    g_one,
    g_mid,
    g_two,
    g_sum,
    g_all,
    s_out,
    s_in,
    update_ref,
    local,
    c_recv,
    c_send,
    v_send,
    v_recv,
    r_send,
    r_recv,
    s_send,
    s_recv,
    small_send,
    small_recv,
):
    me = lax.axis_index("row")
    rank = b_ref.shape[0]
    depth_c, depth_b = c_ref.shape[1], b_ref.shape[1]
    per = k_ref.shape[0] // n
    half = per // 2
    side = 8
    assert depth_c & (depth_c - 1) == 0 and depth_b & (depth_b - 1) == 0
    ring, seat = me // side, me % side
    lane = lax.broadcasted_iota(jnp.int32, (1, 128), 1)
    left = lane < rank

    barrier = pltpu.get_barrier_semaphore()
    home = (me // 2) * 2

    def greet_chip(offset):
        chip = lax.rem(home + offset, n)
        for core in range(2):
            pl.semaphore_signal(barrier, inc=1, device_id={"row": chip + core}, device_id_type=MESH)

    def greet(i, _):
        greet_chip(n // 2 - 2 * i)
        greet_chip(n // 2 + 2 * i)
        return 0

    loads = [
        pltpu.make_async_copy(src, dst, local.at[i])
        for i, (src, dst) in enumerate(
            (
                (count_hbm, count_ref),
                (values_hbm, values_ref),
                (c_hbm, c_ref),
                (k_hbm, k_ref),
                (b_hbm, b_ref),
                (j_hbm, j_ref),
                (w_hbm, w_ref),
                (pick_hbm, pick_ref),
            )
        )
    ]
    for copy in loads:
        copy.start()
    pl.semaphore_signal(barrier, inc=1, device_id={"row": home + 1 - me % 2}, device_id_type=MESH)
    greet_chip(n // 2)
    lax.fori_loop(1, n // 4, greet, 0)

    loads[0].wait()
    loads[1].wait()
    counts = count_ref[...]
    live = jnp.sum(jnp.sum(counts.astype(F32), axis=1, keepdims=True), axis=0, keepdims=True)
    counts = jnp.concatenate([counts, counts], axis=1)

    def mask_values(peer):
        turned = pltpu.roll(counts, 128 - peer, 1)
        for part in range(2):
            kept = lane < turned[part * 8 : part * 8 + 8, 0:1]
            values_out[peer, part] = jnp.where(kept, values_ref[peer, part].astype(F32), 0.0).astype(BF16)

    def send_value(i):
        peer = partner(i, me, n, 1)
        send(values_out.at[peer], values_in.at[me], v_send, v_recv, peer)

    def both(i, _):
        mask_values(partner(i, me, n, 1))
        send_value(i - 1)
        return 0

    mask_values(me)
    values_in[me] = values_out[me]
    mask_values(partner(0, me, n, 1))
    pl.semaphore_wait(barrier, n - 1)
    lax.fori_loop(1, n - 1, both, 0)
    send_value(n - 2)

    def fill(table, ref):
        def chunk(i, _):
            at = pl.multiple_of(i * 128, 128)
            part = ref[:, pl.ds(at, 128)].astype(F32).T
            table[pl.ds(at, 128), :] = jnp.concatenate([part, part], axis=1)
            return 0

        lax.fori_loop(0, ref.shape[1] // 128, chunk, 0)

    def rows_of(table, index_ref, at, mask):
        for i in range(half):
            first = table[pl.ds(index_ref[at + i] & mask, 1), :]
            second = table[pl.ds(index_ref[at + half + i] & mask, 1), :]
            stage[i : i + 1, :] = jnp.where(left, first, second)
        return stage[...]

    loads[2].wait()
    fill(table_c, c_ref)
    loads[3].wait()

    def gather_c(i, _):
        peer = jnp.where(i == n - 1, me, partner(i, me, n, 1))
        c_out[peer] = rows_of(table_c, k_ref, peer * per, depth_c - 1).astype(BF16)
        return 0

    lax.fori_loop(0, n, gather_c, 0)

    def send_c(i, _):
        peer = partner(i, me, n, 1)
        send(c_out.at[peer], c_in.at[me], c_send, c_recv.at[me], peer)
        return 0

    lax.fori_loop(0, n - 1, send_c, 0)

    for copy in loads[4:]:
        copy.wait()
    fill(table_b, b_ref)

    def weigh(i, _):
        turned = w_ref[pl.ds(pl.multiple_of(i * 8, 8), 8), :].T
        for j in range(8):
            wp[i * 8 + j] = jnp.where(left, turned[:half, j : j + 1], turned[half:, j : j + 1])
        return 0

    lax.fori_loop(0, n // 8, weigh, 0)

    def gather_b(e, _):
        wb[e] = rows_of(table_b, j_ref, e * per, depth_b - 1) * wp[e]
        return 0

    lax.fori_loop(0, n, gather_b, 0)

    def use(e, c_rows, gram):
        sketch = wb[e] * c_rows.astype(F32)
        weighted = wp[e] * sketch
        turned = pltpu.roll(weighted, rank, 1)
        at = pl.multiple_of(e * per, 128)
        wk[pl.ds(at, half), :] = jnp.where(left, weighted, turned)
        wk[pl.ds(at + half, half), :] = jnp.where(left, turned, weighted)
        return gram + lax.dot_general(
            sketch, sketch, (((0,), (0,)), ((), ())), precision=HIGHEST, preferred_element_type=F32
        )

    gram = use(me, c_out[me], jnp.zeros((128, 128), F32))

    def take(i, gram):
        e = partner(i, me, n, -1)
        wait_blocks(c_in.at[e], c_send, c_recv.at[e], e, True)
        return use(e, c_in[e], gram)

    gram = lax.fori_loop(0, n - 1, take, gram)

    eye = lax.broadcasted_iota(jnp.int32, (rank, 128), 0) == lax.broadcasted_iota(jnp.int32, (rank, 128), 1)
    square = gram[:rank, :rank] + gram[rank:, rank:]
    system = square * (1.0 / total_samples) + jnp.where(eye[:, :rank], live * (0.05 / total_rows), 0.0)
    packed = jnp.concatenate([system[: rank // 2], system[rank // 2 :]], axis=1)
    lines = packed.shape[0] // side
    for i in range(side):
        g_out[i] = packed[i * lines : (i + 1) * lines]
    g_one[seat] = g_out[seat]

    def spread(kind, src_of, dst, peer_of, own):
        for j in range(1, side):
            peer, index = peer_of(j)
            send(src_of(index), dst.at[own], small_send.at[kind, index], small_recv.at[kind, own], peer)

    def collect(kind, dst, peer_of):
        for j in range(1, side):
            peer, index = peer_of(j)
            wait_blocks(dst.at[index], small_send.at[kind, index], small_recv.at[kind, index], peer, True)

    def in_ring(j):
        index = lax.rem(seat + j, side)
        return ring * side + index, index

    def across(j):
        index = lax.rem(ring + j, side)
        return index * side + seat, index

    def total_of(ref):
        total = ref[0]
        for i in range(1, side):
            total = total + ref[i]
        return total

    spread(0, lambda i: g_out.at[i], g_one, in_ring, seat)

    def pick(q, _):
        for i in range(8):
            first = wk[pl.ds(pick_ref[i, q], 1), :]
            second = wk[pl.ds(pick_ref[8 + i, q], 1), :]
            stage[i : i + 1, :] = jnp.where(left, first, second)
        rows_out[q] = stage[0:8, :].astype(BF16)
        return 0

    lax.fori_loop(0, n, pick, 0)

    collect(0, g_one, in_ring)
    total = total_of(g_one)
    g_mid[...] = total
    g_two[ring] = total
    spread(1, lambda i: g_mid, g_two, across, ring)

    def send_rows(i, _):
        peer = partner(i, me, n, 1)
        send(rows_out.at[peer], rows_in.at[me], r_send, r_recv, peer)
        return 0

    first_part = n * 5 // 8
    lax.fori_loop(0, first_part, send_rows, 0)
    rows_in[me] = rows_out[me]

    collect(1, g_two, across)
    total = total_of(g_two)
    g_sum[...] = total
    g_all[seat] = total
    spread(2, lambda i: g_sum, g_all, in_ring, seat)
    lax.fori_loop(first_part, n - 1, send_rows, 0)
    collect(2, g_all, in_ring)
    packed = jnp.concatenate([g_all[i] for i in range(side)], axis=0)
    matrix = jnp.concatenate([packed, pltpu.roll(packed, rank, 1)], axis=0)
    matrix = jnp.where(left, matrix, pltpu.roll(matrix, rank, 1))

    row_at = lax.broadcasted_iota(jnp.int32, (rank, 1), 0)
    lane_at = lax.rem(lane, rank)

    def eliminate(_, m):
        for i in range(8):
            column = jnp.broadcast_to(m[:, i : i + 1], m.shape)
            line = jnp.where(lane_at == i, 1.0, m[i : i + 1, :]) * (1.0 / column[i : i + 1, :])
            rest = jnp.where(lane_at == i, 0.0, m) - column * line
            m = jnp.where(row_at == i, line, rest)
        m = pltpu.roll(m, 120, 1)
        return jnp.concatenate([m[8:], m[:8]], axis=0)

    inverse = lax.fori_loop(0, rank // 8, eliminate, matrix)[:, :rank]

    far = lax.rem(me + n // 2, n)
    rest = pl.ds(0, n - 1)
    wait_blocks(values_in.at[rest], v_send, v_recv, far, True)
    wait_blocks(rows_in.at[rest], r_send, r_recv, far, True)

    rows = rows_in[...].astype(F32).reshape(n * 8, 128)
    low = values_in[:, 0].astype(F32).reshape(n * 8, 128).astype(BF16)
    high = values_in[:, 1].astype(F32).reshape(n * 8, 128).astype(BF16)
    slot = lax.rem(lax.broadcasted_iota(jnp.int32, (n * 8, 1), 0), 8)

    def mixed(mask, values):
        return lax.dot_general(
            jnp.where(mask, rows, 0.0).astype(BF16), values, (((0,), (0,)), ((), ())), preferred_element_type=F32
        )

    gathered = [
        mixed(slot < 4, low)[:rank],
        mixed(slot >= 4, low)[:rank],
        mixed(slot < 4, high)[rank:],
        mixed(slot >= 4, high)[rank:],
    ]
    squares = jnp.zeros((rank, 128), F32)
    for t, g in enumerate(gathered):
        u = lax.dot_general(inverse, g, (((1,), (0,)), ((), ())), precision=HIGHEST, preferred_element_type=F32)
        update_ref[:, t * 128 : (t + 1) * 128] = u
        squares = squares + u * u
    own = jnp.sum(squares, axis=1, keepdims=True)
    own = jnp.sum(jnp.where(eye, own, 0.0), axis=0, keepdims=True)
    s_out[...] = own
    s_in[me] = own

    def send_sums(i, _):
        peer = partner(i, me, n, 1)
        send(s_out, s_in.at[me], s_send, s_recv, peer)
        return 0

    lax.fori_loop(0, n - 1, send_sums, 0)
    leave = pltpu.make_async_copy(update_ref, update_hbm, local.at[len(loads)])
    leave.start()
    wait_blocks(values_out.at[rest], v_send, v_recv, far, False)
    wait_blocks(c_out.at[rest], c_send, c_recv.at[me], far, False)
    wait_blocks(rows_out.at[rest], r_send, r_recv, far, False)
    for kind, ref, peer_of in ((0, g_out.at[0], in_ring), (1, g_mid, across), (2, g_sum, in_ring)):
        for j in range(1, side):
            peer, index = peer_of(j)
            wait_blocks(ref, small_send.at[kind, index], small_recv.at[kind, index], peer, False)
    leave.wait()
    wait_blocks(s_in.at[rest], s_send, s_recv, far, False)
    wait_blocks(s_in.at[rest], s_send, s_recv, far, True)
    total = jnp.sum(s_in[...], axis=0)
    scales_ref[...] = jnp.sqrt(total / total_rows + 1e-06)


def solution(mesh):
    n = mesh.shape["row"]

    def shards(
        factor_b, factor_c, sample_j, sample_k, sample_weight, block_values, block_sample, block_count
    ):
        rank = factor_b.shape[0]
        samples = sample_j.shape[0]
        _, _, tiles, slots, width = block_values.shape
        values = block_values.reshape(n, 2, tiles * slots // 2, width)
        counts = block_count[0].transpose(1, 2, 0).reshape(tiles * slots, n)
        picks = block_sample[0].transpose(1, 2, 0).reshape(tiles * slots, n)
        weights = sample_weight.reshape(n, -1)
        vmem = pl.BlockSpec(memory_space=pltpu.VMEM)
        anywhere = pl.BlockSpec(memory_space=pl.ANY)
        half = samples // n // 2
        update, scales = pl.pallas_call(
            functools.partial(kernel, n, samples * n, tiles * width * n),
            out_shape=(
                jax.ShapeDtypeStruct((rank, tiles * width), F32),
                jax.ShapeDtypeStruct((1, 128), F32),
            ),
            in_specs=[anywhere] * 8,
            out_specs=(anywhere, vmem),
            scratch_shapes=[
                pltpu.SMEM((samples,), jnp.int32),
                pltpu.SMEM((samples,), jnp.int32),
                pltpu.SMEM(picks.shape, jnp.int32),
                pltpu.VMEM(counts.shape, jnp.int32),
                pltpu.VMEM(factor_b.shape, BF16),
                pltpu.VMEM(factor_c.shape, BF16),
                pltpu.VMEM(weights.shape, F32),
                pltpu.VMEM(values.shape, BF16),
                pltpu.VMEM((factor_c.shape[1], 128), F32),
                pltpu.VMEM((factor_b.shape[1], 128), F32),
                pltpu.VMEM((half, 128), F32),
                pltpu.VMEM((n, half, 128), BF16),
                pltpu.VMEM((n, half, 128), BF16),
                pltpu.VMEM((n, half, 128), F32),
                pltpu.VMEM((n, half, 128), F32),
                pltpu.VMEM((samples, 128), F32),
                pltpu.VMEM(values.shape, BF16),
                pltpu.VMEM(values.shape, BF16),
                pltpu.VMEM((n, 8, 128), BF16),
                pltpu.VMEM((n, 8, 128), BF16),
                pltpu.VMEM((8, 4, 128), F32),
                pltpu.VMEM((8, 4, 128), F32),
                pltpu.VMEM((4, 128), F32),
                pltpu.VMEM((8, 4, 128), F32),
                pltpu.VMEM((4, 128), F32),
                pltpu.VMEM((8, 4, 128), F32),
                pltpu.VMEM((1, 128), F32),
                pltpu.VMEM((n, 1, 128), F32),
                pltpu.VMEM((rank, tiles * width), F32),
                pltpu.SemaphoreType.DMA((9,)),
                pltpu.SemaphoreType.DMA((n,)),
            ]
            + [pltpu.SemaphoreType.DMA(())] * 7
            + [pltpu.SemaphoreType.DMA((3, 8))] * 2,
            compiler_params=pltpu.CompilerParams(collective_id=0, has_side_effects=True),
            name="step",
        )(
            sample_k.reshape(-1),
            sample_j,
            picks,
            counts,
            factor_b,
            factor_c,
            weights,
            values,
        )
        scales = scales[0, :rank]
        return (update / scales[:, None]).astype(BF16), scales

    return jax.shard_map(
        shards,
        mesh=mesh,
        in_specs=(
            P(None, GROUPS_ROW),
            P(None, GROUPS_ROW),
            P(GROUPS_ROW),
            P(None, GROUPS_ROW, None),
            P(GROUPS_ROW),
            P(GROUPS_ROW, None, None, None, None),
            P(GROUPS_ROW, None, None, None),
            P(GROUPS_ROW, None, None, None),
        ),
        out_specs=(P(None, GROUPS_ROW), P("groups")),
        check_vma=False,
    )
```

time: 212 us -> 197 us (0.929)
  Pallas kernels: 204 us -> 194 us
  local copies, waits for them, and re-layouts: 4.3 us -> 0.62 us
    pallas_call x1, Pallas kernels: 204 us -> 194 us  [shards(): pl.pallas_call(functools.partial(kernel, n, samples * n, tiles * width *...]
where the time goes in v2:
time: 197 us
  Pallas kernels  194 us (98%)
    pallas_call x1, Pallas kernels, shards(): pl.pallas_call(functools.partial(kernel, n, samples * n, tiles * width *...  194 us

profile of v2, /device:TPU:37, one launch (start us, length us, event | category | flops | bytes accessed | tf_op | source)
XLA Modules:
  0.0 196.9 jit_solution(1568650620160329812)
XLA Ops:
  0.6 194.0 %step.1 = (f32[64,512]{1,0:T(8,128)}, f32[1,128]{1,0:T(1,128)}) custom-call(s32[8192]{0:T(1024)} %bitcast.16, s32[8192]{0:T(1024)} %j_hbm.1, s32[16,64]{1,0:T(8,128)} %bitcast.18, s32[16,64]{1,0:T(8,128)} %bitcast.19, bf16[64,4096]{1,0:T(8,128)(2,1)} %b_hbm.1, bf16[64,4096]{1,0:T(8,128)(2,1)} %c_hbm.1, f32[64,128]{1,0:T(8,128)} %bitcast.17, ...), custom_call_target="tpu_custom_call" | custom-call | tf_op jit(solution)/shard_map/step/pallas_call | solution.py:404
  194.7 0.0 copy-start.1
  194.7 0.6 copy-done.1
  195.3 0.0 copy-start
  195.3 1.6 divide_convert_fusion
  196.9 0.0 copy-done
  (1 shorter events, 0.0 us)
Async XLA Ops:
  194.7 0.6 copy-start.1
  195.3 1.6 copy-start

commit v3 on v2

--- a/solution.py
+++ b/solution.py
@@ -143,37 +143,9 @@
     ]
     for copy in loads:
         copy.start()
-    pl.semaphore_signal(barrier, inc=1, device_id={"row": home + 1 - me % 2}, device_id_type=MESH)
     greet_chip(n // 2)
     lax.fori_loop(1, n // 4, greet, 0)
-
-    loads[0].wait()
-    loads[1].wait()
-    counts = count_ref[...]
-    live = jnp.sum(jnp.sum(counts.astype(F32), axis=1, keepdims=True), axis=0, keepdims=True)
-    counts = jnp.concatenate([counts, counts], axis=1)
-
-    def mask_values(peer):
-        turned = pltpu.roll(counts, 128 - peer, 1)
-        for part in range(2):
-            kept = lane < turned[part * 8 : part * 8 + 8, 0:1]
-            values_out[peer, part] = jnp.where(kept, values_ref[peer, part].astype(F32), 0.0).astype(BF16)
-
-    def send_value(i):
-        peer = partner(i, me, n, 1)
-        send(values_out.at[peer], values_in.at[me], v_send, v_recv, peer)
-
-    def both(i, _):
-        mask_values(partner(i, me, n, 1))
-        send_value(i - 1)
-        return 0
-
-    mask_values(me)
-    values_in[me] = values_out[me]
-    mask_values(partner(0, me, n, 1))
-    pl.semaphore_wait(barrier, n - 1)
-    lax.fori_loop(1, n - 1, both, 0)
-    send_value(n - 2)
+    pl.semaphore_signal(barrier, inc=1, device_id={"row": home + 1 - me % 2}, device_id_type=MESH)
 
     def fill(table, ref):
         def chunk(i, _):
@@ -191,8 +163,62 @@
             stage[i : i + 1, :] = jnp.where(left, first, second)
         return stage[...]
 
+    loads[0].wait()
+    loads[1].wait()
+    counts = count_ref[...]
+    live = jnp.sum(jnp.sum(counts.astype(F32), axis=1, keepdims=True), axis=0, keepdims=True)
+    counts = jnp.concatenate([counts, counts], axis=1)
+
+    def mask_values(peer):
+        turned = pltpu.roll(counts, 128 - peer, 1)
+        for part in range(2):
+            kept = lane < turned[part * 8 : part * 8 + 8, 0:1]
+            values_out[peer, part] = jnp.where(kept, values_ref[peer, part].astype(F32), 0.0).astype(BF16)
+
+    far = [lax.rem(home + n // 2, n), lax.rem(home + n // 2, n) + 1]
+    mate = home + 1 - me % 2
+    reach = n // 4 - 1
+
+    def peers(dist):
+        up = lax.rem(home + 2 * dist, n)
+        down = lax.rem(home + n - 2 * dist, n)
+        return up, up + 1, down, down + 1
+
+    def by_distance(high, low, act):
+        def body(i, _):
+            for peer in peers(high - i):
+                act(peer)
+            return 0
+
+        lax.fori_loop(0, high - low + 1, body, 0)
+
+    def send_value(peer):
+        send(values_out.at[peer], values_in.at[me], v_send, v_recv, peer)
+
+    early = reach - 3
+
+    def both(i, _):
+        for peer in peers(reach - i):
+            mask_values(peer)
+        for peer in peers(reach - i + 1):
+            send_value(peer)
+        return 0
+
+    mask_values(me)
+    values_in[me] = values_out[me]
+    for peer in far:
+        mask_values(peer)
     loads[2].wait()
     fill(table_c, c_ref)
+    pl.semaphore_wait(barrier, n - 1)
+    for peer in peers(reach):
+        mask_values(peer)
+    for peer in far:
+        send_value(peer)
+    lax.fori_loop(1, reach - early + 1, both, 0)
+    for peer in peers(early):
+        send_value(peer)
+
     loads[3].wait()
 
     def gather_c(i, _):
@@ -202,12 +228,15 @@
 
     lax.fori_loop(0, n, gather_c, 0)
 
-    def send_c(i, _):
-        peer = partner(i, me, n, 1)
+    def send_c(peer):
         send(c_out.at[peer], c_in.at[me], c_send, c_recv.at[me], peer)
-        return 0
-
-    lax.fori_loop(0, n - 1, send_c, 0)
+
+    for peer in far:
+        send_c(peer)
+    by_distance(reach, 1, send_c)
+    send_c(mate)
+    by_distance(early - 1, 1, mask_values)
+    mask_values(mate)
 
     for copy in loads[4:]:
         copy.wait()
@@ -281,6 +310,8 @@
         return total
 
     spread(0, lambda i: g_out.at[i], g_one, in_ring, seat)
+    middle = early - 2
+    by_distance(early - 1, middle, send_value)
 
     def pick(q, _):
         for i in range(8):
@@ -298,13 +329,14 @@
     g_two[ring] = total
     spread(1, lambda i: g_mid, g_two, across, ring)
 
-    def send_rows(i, _):
-        peer = partner(i, me, n, 1)
+    def send_rows(peer):
         send(rows_out.at[peer], rows_in.at[me], r_send, r_recv, peer)
-        return 0
-
-    first_part = n * 5 // 8
-    lax.fori_loop(0, first_part, send_rows, 0)
+
+    by_distance(middle - 1, 1, send_value)
+    send_value(mate)
+    for peer in far:
+        send_rows(peer)
+    by_distance(reach, reach, send_rows)
     rows_in[me] = rows_out[me]
 
     collect(1, g_two, across)
@@ -312,7 +344,8 @@
     g_sum[...] = total
     g_all[seat] = total
     spread(2, lambda i: g_sum, g_all, in_ring, seat)
-    lax.fori_loop(first_part, n - 1, send_rows, 0)
+    by_distance(reach - 1, 1, send_rows)
+    send_rows(mate)
     collect(2, g_all, in_ring)
     packed = jnp.concatenate([g_all[i] for i in range(side)], axis=0)
     matrix = jnp.concatenate([packed, pltpu.roll(packed, rank, 1)], axis=0)
@@ -322,20 +355,26 @@
     lane_at = lax.rem(lane, rank)
 
     def eliminate(_, m):
-        for i in range(8):
-            column = jnp.broadcast_to(m[:, i : i + 1], m.shape)
-            line = jnp.where(lane_at == i, 1.0, m[i : i + 1, :]) * (1.0 / column[i : i + 1, :])
-            rest = jnp.where(lane_at == i, 0.0, m) - column * line
-            m = jnp.where(row_at == i, line, rest)
+        for i in range(0, 8, 2):
+            one = jnp.broadcast_to(m[:, i : i + 1], m.shape)
+            two = jnp.broadcast_to(m[:, i + 1 : i + 2], m.shape)
+            a, b = one[i : i + 1, :], one[i + 1 : i + 2, :]
+            c, d = two[i : i + 1, :], two[i + 1 : i + 2, :]
+            scale = 1.0 / (a * d - b * c)
+            upper = jnp.where(lane_at == i, 1.0, jnp.where(lane_at == i + 1, 0.0, m[i : i + 1, :]))
+            lower = jnp.where(lane_at == i, 0.0, jnp.where(lane_at == i + 1, 1.0, m[i + 1 : i + 2, :]))
+            first = (d * scale) * upper - (c * scale) * lower
+            second = (a * scale) * lower - (b * scale) * upper
+            rest = jnp.where(lane_at // 2 == i // 2, 0.0, m) - one * first - two * second
+            m = jnp.where(row_at == i, first, jnp.where(row_at == i + 1, second, rest))
         m = pltpu.roll(m, 120, 1)
         return jnp.concatenate([m[8:], m[:8]], axis=0)
 
     inverse = lax.fori_loop(0, rank // 8, eliminate, matrix)[:, :rank]
 
-    far = lax.rem(me + n // 2, n)
     rest = pl.ds(0, n - 1)
-    wait_blocks(values_in.at[rest], v_send, v_recv, far, True)
-    wait_blocks(rows_in.at[rest], r_send, r_recv, far, True)
+    wait_blocks(values_in.at[rest], v_send, v_recv, mate, True)
+    wait_blocks(rows_in.at[rest], r_send, r_recv, mate, True)
 
     rows = rows_in[...].astype(F32).reshape(n * 8, 128)
     low = values_in[:, 0].astype(F32).reshape(n * 8, 128).astype(BF16)
@@ -363,24 +402,25 @@
     s_out[...] = own
     s_in[me] = own
 
-    def send_sums(i, _):
-        peer = partner(i, me, n, 1)
+    def send_sums(peer):
         send(s_out, s_in.at[me], s_send, s_recv, peer)
-        return 0
-
-    lax.fori_loop(0, n - 1, send_sums, 0)
+
+    for peer in far:
+        send_sums(peer)
+    by_distance(reach, 1, send_sums)
+    send_sums(mate)
     leave = pltpu.make_async_copy(update_ref, update_hbm, local.at[len(loads)])
     leave.start()
-    wait_blocks(values_out.at[rest], v_send, v_recv, far, False)
-    wait_blocks(c_out.at[rest], c_send, c_recv.at[me], far, False)
-    wait_blocks(rows_out.at[rest], r_send, r_recv, far, False)
+    wait_blocks(values_out.at[rest], v_send, v_recv, mate, False)
+    wait_blocks(c_out.at[rest], c_send, c_recv.at[me], mate, False)
+    wait_blocks(rows_out.at[rest], r_send, r_recv, mate, False)
     for kind, ref, peer_of in ((0, g_out.at[0], in_ring), (1, g_mid, across), (2, g_sum, in_ring)):
         for j in range(1, side):
             peer, index = peer_of(j)
             wait_blocks(ref, small_send.at[kind, index], small_recv.at[kind, index], peer, False)
     leave.wait()
-    wait_blocks(s_in.at[rest], s_send, s_recv, far, False)
-    wait_blocks(s_in.at[rest], s_send, s_recv, far, True)
+    wait_blocks(s_in.at[rest], s_send, s_recv, mate, False)
+    wait_blocks(s_in.at[rest], s_send, s_recv, mate, True)
     total = jnp.sum(s_in[...], axis=0)
     scales_ref[...] = jnp.sqrt(total / total_rows + 1e-06)
 

time: 197 us -> 189 us (0.959)
  Pallas kernels: 194 us -> 186 us
    pallas_call x1, Pallas kernels: 194 us -> 186 us  [shards(): pl.pallas_call(functools.partial(kernel, n, samples * n, tiles * width *...]
where the time goes in v3:
time: 189 us
  Pallas kernels  186 us (98%)
    pallas_call x1, Pallas kernels, shards(): pl.pallas_call(functools.partial(kernel, n, samples * n, tiles * width *...  186 us

profile of v3, /device:TPU:37, one launch (start us, length us, event | category | flops | bytes accessed | tf_op | source)
XLA Modules:
  0.0 188.5 jit_solution(10414214289882736996)
XLA Ops:
  0.6 185.6 %step.1 = (f32[64,512]{1,0:T(8,128)}, f32[1,128]{1,0:T(1,128)}) custom-call(s32[8192]{0:T(1024)} %bitcast.16, s32[8192]{0:T(1024)} %j_hbm.1, s32[16,64]{1,0:T(8,128)} %bitcast.18, s32[16,64]{1,0:T(8,128)} %bitcast.19, bf16[64,4096]{1,0:T(8,128)(2,1)} %b_hbm.1, bf16[64,4096]{1,0:T(8,128)(2,1)} %c_hbm.1, f32[64,128]{1,0:T(8,128)} %bitcast.17, ...), custom_call_target="tpu_custom_call" | custom-call | tf_op jit(solution)/shard_map/step/pallas_call | solution.py:444
  186.3 0.0 copy-start.1
  186.3 0.6 copy-done.1
  186.9 0.0 copy-start
  186.9 1.6 divide_convert_fusion
  188.5 0.0 copy-done
  (1 shorter events, 0.0 us)
Async XLA Ops:
  186.3 0.6 copy-start.1
  186.9 1.6 copy-start

commit v4 on v3

--- a/solution.py
+++ b/solution.py
@@ -77,10 +77,8 @@
     wb,
     wp,
     wk,
-    values_out,
-    values_in,
-    rows_out,
-    rows_in,
+    block_out,
+    block_in,
     g_out,
     g_one,
     g_mid,
@@ -93,10 +91,8 @@
     local,
     c_recv,
     c_send,
-    v_send,
-    v_recv,
-    r_send,
-    r_recv,
+    b_send,
+    b_recv,
     s_send,
     s_recv,
     small_send,
@@ -149,12 +145,13 @@
 
     def fill(table, ref):
         def chunk(i, _):
-            at = pl.multiple_of(i * 128, 128)
-            part = ref[:, pl.ds(at, 128)].astype(F32).T
-            table[pl.ds(at, 128), :] = jnp.concatenate([part, part], axis=1)
+            for j in range(4):
+                at = pl.multiple_of(i * 512 + j * 128, 128)
+                part = ref[:, pl.ds(at, 128)].astype(F32)
+                table[pl.ds(at, 128), :] = jnp.concatenate([part, part], axis=0).T
             return 0
 
-        lax.fori_loop(0, ref.shape[1] // 128, chunk, 0)
+        lax.fori_loop(0, ref.shape[1] // 512, chunk, 0)
 
     def rows_of(table, index_ref, at, mask):
         for i in range(half):
@@ -173,7 +170,7 @@
         turned = pltpu.roll(counts, 128 - peer, 1)
         for part in range(2):
             kept = lane < turned[part * 8 : part * 8 + 8, 0:1]
-            values_out[peer, part] = jnp.where(kept, values_ref[peer, part].astype(F32), 0.0).astype(BF16)
+            block_out[peer, part] = jnp.where(kept, values_ref[peer, part].astype(F32), 0.0).astype(BF16)
 
     far = [lax.rem(home + n // 2, n), lax.rem(home + n // 2, n) + 1]
     mate = home + 1 - me % 2
@@ -193,9 +190,16 @@
         lax.fori_loop(0, high - low + 1, body, 0)
 
     def send_value(peer):
-        send(values_out.at[peer], values_in.at[me], v_send, v_recv, peer)
-
-    early = reach - 3
+        pair = pl.ds(0, 2)
+        send(block_out.at[peer, pair], block_in.at[me, pair], b_send, b_recv, peer)
+
+    def send_rows(peer):
+        send(block_out.at[peer, 2], block_in.at[me, 2], b_send, b_recv, peer)
+
+    def send_block(peer):
+        send(block_out.at[peer], block_in.at[me], b_send, b_recv, peer)
+
+    early = reach - 5
 
     def both(i, _):
         for peer in peers(reach - i):
@@ -205,11 +209,8 @@
         return 0
 
     mask_values(me)
-    values_in[me] = values_out[me]
     for peer in far:
         mask_values(peer)
-    loads[2].wait()
-    fill(table_c, c_ref)
     pl.semaphore_wait(barrier, n - 1)
     for peer in peers(reach):
         mask_values(peer)
@@ -219,21 +220,24 @@
     for peer in peers(early):
         send_value(peer)
 
+    loads[2].wait()
+    fill(table_c, c_ref)
     loads[3].wait()
 
-    def gather_c(i, _):
-        peer = jnp.where(i == n - 1, me, partner(i, me, n, 1))
+    def gather_c(peer):
         c_out[peer] = rows_of(table_c, k_ref, peer * per, depth_c - 1).astype(BF16)
-        return 0
-
-    lax.fori_loop(0, n, gather_c, 0)
 
     def send_c(peer):
         send(c_out.at[peer], c_in.at[me], c_send, c_recv.at[me], peer)
 
-    for peer in far:
-        send_c(peer)
-    by_distance(reach, 1, send_c)
+    def gather_and_send(i, _):
+        gather_c(partner(i, me, n, 1))
+        send_c(partner(i - 1, me, n, 1))
+        return 0
+
+    gather_c(far[0])
+    lax.fori_loop(1, n - 1, gather_and_send, 0)
+    gather_c(me)
     send_c(mate)
     by_distance(early - 1, 1, mask_values)
     mask_values(mate)
@@ -310,18 +314,19 @@
         return total
 
     spread(0, lambda i: g_out.at[i], g_one, in_ring, seat)
-    middle = early - 2
-    by_distance(early - 1, middle, send_value)
-
     def pick(q, _):
         for i in range(8):
             first = wk[pl.ds(pick_ref[i, q], 1), :]
             second = wk[pl.ds(pick_ref[8 + i, q], 1), :]
             stage[i : i + 1, :] = jnp.where(left, first, second)
-        rows_out[q] = stage[0:8, :].astype(BF16)
+        block_out[q, 2] = stage[0:8, :].astype(BF16)
         return 0
 
     lax.fori_loop(0, n, pick, 0)
+    for peer in far:
+        send_rows(peer)
+    by_distance(reach, reach, send_rows)
+    block_in[me] = block_out[me]
 
     collect(0, g_one, in_ring)
     total = total_of(g_one)
@@ -329,23 +334,16 @@
     g_two[ring] = total
     spread(1, lambda i: g_mid, g_two, across, ring)
 
-    def send_rows(peer):
-        send(rows_out.at[peer], rows_in.at[me], r_send, r_recv, peer)
-
-    by_distance(middle - 1, 1, send_value)
-    send_value(mate)
-    for peer in far:
-        send_rows(peer)
-    by_distance(reach, reach, send_rows)
-    rows_in[me] = rows_out[me]
-
+    middle = early - 3
+    by_distance(reach - 1, early, send_rows)
+    by_distance(early - 1, middle, send_block)
     collect(1, g_two, across)
     total = total_of(g_two)
     g_sum[...] = total
     g_all[seat] = total
     spread(2, lambda i: g_sum, g_all, in_ring, seat)
-    by_distance(reach - 1, 1, send_rows)
-    send_rows(mate)
+    by_distance(middle - 1, 1, send_block)
+    send_block(mate)
     collect(2, g_all, in_ring)
     packed = jnp.concatenate([g_all[i] for i in range(side)], axis=0)
     matrix = jnp.concatenate([packed, pltpu.roll(packed, rank, 1)], axis=0)
@@ -373,12 +371,11 @@
     inverse = lax.fori_loop(0, rank // 8, eliminate, matrix)[:, :rank]
 
     rest = pl.ds(0, n - 1)
-    wait_blocks(values_in.at[rest], v_send, v_recv, mate, True)
-    wait_blocks(rows_in.at[rest], r_send, r_recv, mate, True)
-
-    rows = rows_in[...].astype(F32).reshape(n * 8, 128)
-    low = values_in[:, 0].astype(F32).reshape(n * 8, 128).astype(BF16)
-    high = values_in[:, 1].astype(F32).reshape(n * 8, 128).astype(BF16)
+    wait_blocks(block_in.at[rest], b_send, b_recv, mate, True)
+
+    rows = block_in[:, 2].astype(F32).reshape(n * 8, 128)
+    low = block_in[:, 0].astype(F32).reshape(n * 8, 128).astype(BF16)
+    high = block_in[:, 1].astype(F32).reshape(n * 8, 128).astype(BF16)
     slot = lax.rem(lax.broadcasted_iota(jnp.int32, (n * 8, 1), 0), 8)
 
     def mixed(mask, values):
@@ -411,9 +408,8 @@
     send_sums(mate)
     leave = pltpu.make_async_copy(update_ref, update_hbm, local.at[len(loads)])
     leave.start()
-    wait_blocks(values_out.at[rest], v_send, v_recv, mate, False)
+    wait_blocks(block_out.at[rest], b_send, b_recv, mate, False)
     wait_blocks(c_out.at[rest], c_send, c_recv.at[me], mate, False)
-    wait_blocks(rows_out.at[rest], r_send, r_recv, mate, False)
     for kind, ref, peer_of in ((0, g_out.at[0], in_ring), (1, g_mid, across), (2, g_sum, in_ring)):
         for j in range(1, side):
             peer, index = peer_of(j)
@@ -466,10 +462,8 @@
                 pltpu.VMEM((n, half, 128), F32),
                 pltpu.VMEM((n, half, 128), F32),
                 pltpu.VMEM((samples, 128), F32),
-                pltpu.VMEM(values.shape, BF16),
-                pltpu.VMEM(values.shape, BF16),
-                pltpu.VMEM((n, 8, 128), BF16),
-                pltpu.VMEM((n, 8, 128), BF16),
+                pltpu.VMEM((n, 3, 8, 128), BF16),
+                pltpu.VMEM((n, 3, 8, 128), BF16),
                 pltpu.VMEM((8, 4, 128), F32),
                 pltpu.VMEM((8, 4, 128), F32),
                 pltpu.VMEM((4, 128), F32),
@@ -482,7 +476,7 @@
                 pltpu.SemaphoreType.DMA((9,)),
                 pltpu.SemaphoreType.DMA((n,)),
             ]
-            + [pltpu.SemaphoreType.DMA(())] * 7
+            + [pltpu.SemaphoreType.DMA(())] * 5
             + [pltpu.SemaphoreType.DMA((3, 8))] * 2,
             compiler_params=pltpu.CompilerParams(collective_id=0, has_side_effects=True),
             name="step",

time: 189 us -> 185 us (0.979)
  Pallas kernels: 186 us -> 182 us
    pallas_call x1, Pallas kernels: 186 us -> 182 us  [shards(): pl.pallas_call(functools.partial(kernel, n, samples * n, tiles * width *...]
where the time goes in v4:
time: 185 us
  Pallas kernels  182 us (98%)
    pallas_call x1, Pallas kernels, shards(): pl.pallas_call(functools.partial(kernel, n, samples * n, tiles * width *...  182 us

profile of v4, /device:TPU:37, one launch (start us, length us, event | category | flops | bytes accessed | tf_op | source)
XLA Modules:
  0.0 184.8 jit_solution(10786408628794983872)
XLA Ops:
  0.6 181.9 %step.1 = (f32[64,512]{1,0:T(8,128)}, f32[1,128]{1,0:T(1,128)}) custom-call(s32[8192]{0:T(1024)} %bitcast.16, s32[8192]{0:T(1024)} %j_hbm.1, s32[16,64]{1,0:T(8,128)} %bitcast.18, s32[16,64]{1,0:T(8,128)} %bitcast.19, bf16[64,4096]{1,0:T(8,128)(2,1)} %b_hbm.1, bf16[64,4096]{1,0:T(8,128)(2,1)} %c_hbm.1, f32[64,128]{1,0:T(8,128)} %bitcast.17, ...), custom_call_target="tpu_custom_call" | custom-call | tf_op jit(solution)/shard_map/step/pallas_call | solution.py:440
  182.5 0.0 copy-start.1
  182.5 0.6 copy-done.1
  183.2 0.0 copy-start
  183.2 1.6 divide_convert_fusion
  184.8 0.0 copy-done
  (1 shorter events, 0.0 us)
Async XLA Ops:
  182.5 0.6 copy-start.1
  183.2 1.6 copy-start

commit v5 on v4

--- a/solution.py
+++ b/solution.py
@@ -353,18 +353,27 @@
     lane_at = lax.rem(lane, rank)
 
     def eliminate(_, m):
-        for i in range(0, 8, 2):
-            one = jnp.broadcast_to(m[:, i : i + 1], m.shape)
-            two = jnp.broadcast_to(m[:, i + 1 : i + 2], m.shape)
-            a, b = one[i : i + 1, :], one[i + 1 : i + 2, :]
-            c, d = two[i : i + 1, :], two[i + 1 : i + 2, :]
-            scale = 1.0 / (a * d - b * c)
-            upper = jnp.where(lane_at == i, 1.0, jnp.where(lane_at == i + 1, 0.0, m[i : i + 1, :]))
-            lower = jnp.where(lane_at == i, 0.0, jnp.where(lane_at == i + 1, 1.0, m[i + 1 : i + 2, :]))
-            first = (d * scale) * upper - (c * scale) * lower
-            second = (a * scale) * lower - (b * scale) * upper
-            rest = jnp.where(lane_at // 2 == i // 2, 0.0, m) - one * first - two * second
-            m = jnp.where(row_at == i, first, jnp.where(row_at == i + 1, second, rest))
+        for start in range(0, 8, 4):
+            columns = [jnp.broadcast_to(m[:, start + t : start + t + 1], m.shape) for t in range(4)]
+            for t in range(0, 4, 2):
+                i = start + t
+                one, two = columns[t], columns[t + 1]
+                a, b = one[i : i + 1, :], one[i + 1 : i + 2, :]
+                c, d = two[i : i + 1, :], two[i + 1 : i + 2, :]
+                scale = 1.0 / (a * d - b * c)
+                a, b, c, d = a * scale, b * scale, c * scale, d * scale
+
+                def solved(upper, lower, others):
+                    first, second = d * upper - c * lower, a * lower - b * upper
+                    rest = others - one * first - two * second
+                    return jnp.where(row_at == i, first, jnp.where(row_at == i + 1, second, rest))
+
+                for later in range(t + 2, 4):
+                    x = columns[later]
+                    columns[later] = solved(x[i : i + 1, :], x[i + 1 : i + 2, :], x)
+                upper = jnp.where(lane_at == i, 1.0, jnp.where(lane_at == i + 1, 0.0, m[i : i + 1, :]))
+                lower = jnp.where(lane_at == i, 0.0, jnp.where(lane_at == i + 1, 1.0, m[i + 1 : i + 2, :]))
+                m = solved(upper, lower, jnp.where(lane_at // 2 == i // 2, 0.0, m))
         m = pltpu.roll(m, 120, 1)
         return jnp.concatenate([m[8:], m[:8]], axis=0)
 

time: 185 us -> 185 us (level)
  no operation moved by 1% of the time
where the time goes in v5:
time: 185 us
  Pallas kernels  182 us (98%)
    pallas_call x1, Pallas kernels, shards(): pl.pallas_call(functools.partial(kernel, n, samples * n, tiles * width *...  182 us

profile of v5, /device:TPU:37, one launch (start us, length us, event | category | flops | bytes accessed | tf_op | source)
XLA Modules:
  0.0 184.8 jit_solution(16649051374275647471)
XLA Ops:
  0.6 181.9 %step.1 = (f32[64,512]{1,0:T(8,128)}, f32[1,128]{1,0:T(1,128)}) custom-call(s32[8192]{0:T(1024)} %bitcast.16, s32[8192]{0:T(1024)} %j_hbm.1, s32[16,64]{1,0:T(8,128)} %bitcast.18, s32[16,64]{1,0:T(8,128)} %bitcast.19, bf16[64,4096]{1,0:T(8,128)(2,1)} %b_hbm.1, bf16[64,4096]{1,0:T(8,128)(2,1)} %c_hbm.1, f32[64,128]{1,0:T(8,128)} %bitcast.17, ...), custom_call_target="tpu_custom_call" | custom-call | tf_op jit(solution)/shard_map/step/pallas_call | solution.py:449
  182.5 0.0 copy-start.1
  182.5 0.6 copy-done.1
  183.2 0.0 copy-start
  183.2 1.6 divide_convert_fusion
  184.8 0.0 copy-done
  (1 shorter events, 0.0 us)
Async XLA Ops:
  182.5 0.6 copy-start.1
  183.2 1.6 copy-start
